TPU v7x, 32 devices: a whole 2x2x4 slice. The times are simulated.
32 devices in a mesh: tm: 8 (over z, y), space: 4 (over x, core).
Axes of the slice: x: 2, y: 2, z: 4, core: 2. Of those that a mesh axis runs over, the one named last changes fastest.
Arguments:
- starts: float32 [8, 5, 16, 64, 128], P('tm', None, 'space'), may hold values from -4 to 4
- source: float32 [5, 16, 64, 128], P(None, 'space'), may hold values from -4 to 4
Outputs:
- ends: float32 [8, 5, 16, 64, 128], P('tm', None, 'space')
- slice_norms: float32 [8], P('tm')
- total_norm: float32 [1], replicated
All inputs are finite; a program needn't handle non-finite values.
Results may differ from a plain program's by a relative error of at most 0.0003.
Values sent between devices are 32-bit elements; how exact they have to be, the bound alone decides.
A program may use at most 64 MiB of HBM per device.

v0:
```python
import math
import jax
import jax.numpy as jnp
from jax import lax
from jax.sharding import PartitionSpec as P

viscosity = 0.08
diffusivity = 0.05
compress_rate = 0.25
time_step = 0.5
diffusion_number = 0.08
advect_xaxis = 0.2
advect_yaxis = 0.15
advect_zaxis = 0.1
epsilon = 1e-06
highest = lax.Precision.HIGHEST


def with_halo(cells, sides, width):
    for axis, dim in sides:
        count = lax.axis_size(axis)
        head = lax.slice_in_dim(cells, 0, width, axis=dim)
        tail = lax.slice_in_dim(cells, cells.shape[dim] - width, cells.shape[dim], axis=dim)
        cells = jnp.concatenate(
            [
                lax.ppermute(tail, axis, [(i, (i + 1) % count) for i in range(count)]),
                cells,
                lax.ppermute(head, axis, [((i + 1) % count, i) for i in range(count)]),
            ],
            axis=dim,
        )
    return cells


def across(values, axis):
    return 0.5 * (jnp.roll(values, -1, axis) - jnp.roll(values, 1, axis))


def vertical(values):
    return 0.5 * (values[2:] - values[:-2])


def laplace(values):
    interior = values[1:-1]
    summed = values[2:] + values[:-2] - 6.0 * interior
    for axis in (1, 2):
        summed = summed + jnp.roll(interior, -1, axis) + jnp.roll(interior, 1, axis)
    return summed


def tendency(padded, source):
    speed_xaxis = advect_xaxis + padded[0]
    speed_yaxis = advect_yaxis + padded[1]
    speed_zaxis = advect_zaxis + padded[2]

    def transport(quantity):
        return (
            across((speed_xaxis * quantity)[1:-1], 2)
            + across((speed_yaxis * quantity)[1:-1], 1)
            + vertical(speed_zaxis * quantity)
        )

    pressure = padded[3]
    xmomentum = -transport(padded[0]) - across(pressure[1:-1], 2) + viscosity * laplace(padded[0])
    ymomentum = -transport(padded[1]) - across(pressure[1:-1], 1) + viscosity * laplace(padded[1])
    zmomentum = -transport(padded[2]) - vertical(pressure) + viscosity * laplace(padded[2])
    pressure_rate = -compress_rate * (
        across(padded[0][1:-1], 2) + across(padded[1][1:-1], 1) + vertical(padded[2])
    )
    scalar_rate = -transport(padded[4]) + diffusivity * laplace(padded[4])
    return jnp.stack([xmomentum, ymomentum, zmomentum, pressure_rate, scalar_rate]) + source


def slab_rates(current, source):
    padded = with_halo(current, (("space", 1),), 1)
    return tendency(padded, source)


def kept_modes(keep):
    mode_ids = jnp.arange(2 * keep, dtype=jnp.int32)
    return jnp.where(mode_ids < keep, mode_ids, mode_ids - 2 * keep)


def wave_table(cell_ids, mode_ids, length):
    products = cell_ids[:, None] * mode_ids[None, :] % length
    angles = 2.0 * math.pi / length * products.astype(jnp.float32)
    return (jnp.cos(angles), jnp.sin(angles))


def shards(starts, source):
    state_now = starts[0]
    fields, slab_depth, grid_rows, grid_cols = state_now.shape
    width_space = lax.axis_size("space")
    width_time = lax.axis_size("tm")
    grid_depth = slab_depth * width_space
    keep_y = grid_rows // 8
    keep_x = grid_cols // 16
    mode_count = 4 * keep_y * keep_x
    current = state_now
    section_one = slab_rates(current, source)
    section_two = slab_rates(current + 0.5 * time_step * section_one, source)
    section_three = slab_rates(current + 0.5 * time_step * section_two, source)
    section_four = slab_rates(current + time_step * section_three, source)
    current = current + time_step / 6.0 * (
        section_one + 2.0 * section_two + 2.0 * section_three + section_four
    )
    xmodes = kept_modes(keep_x)
    ymodes = kept_modes(keep_y)
    xcosines, xsines = wave_table(jnp.arange(grid_cols, dtype=jnp.int32), xmodes, grid_cols)
    ycosines, ysines = wave_table(jnp.arange(grid_rows, dtype=jnp.int32), ymodes, grid_rows)
    stacked = jnp.stack([current, state_now]).reshape(2 * fields, slab_depth, grid_rows, grid_cols)
    real_x = jnp.einsum("bzyx,xk->bzyk", stacked, xcosines, precision=highest)
    imag_x = -jnp.einsum("bzyx,xk->bzyk", stacked, xsines, precision=highest)
    real_y = jnp.einsum("bzyk,yj->bzjk", real_x, ycosines, precision=highest) + jnp.einsum(
        "bzyk,yj->bzjk", imag_x, ysines, precision=highest
    )
    imag_y = jnp.einsum("bzyk,yj->bzjk", imag_x, ycosines, precision=highest) - jnp.einsum(
        "bzyk,yj->bzjk", real_x, ysines, precision=highest
    )
    real_y = real_y.reshape(2 * fields, slab_depth, mode_count)
    imag_y = imag_y.reshape(2 * fields, slab_depth, mode_count)
    space_pos = lax.axis_index("space")
    zcells = space_pos * slab_depth + jnp.arange(slab_depth, dtype=jnp.int32)
    zwaves = jnp.arange(lax.axis_size("space") * slab_depth, dtype=jnp.int32)
    zcosines, zsines = wave_table(zwaves, zcells, grid_depth)
    term_real = jnp.einsum("qz,bzm->qbm", zcosines, real_y, precision=highest) + jnp.einsum(
        "qz,bzm->qbm", zsines, imag_y, precision=highest
    )
    term_imag = jnp.einsum("qz,bzm->qbm", zcosines, imag_y, precision=highest) - jnp.einsum(
        "qz,bzm->qbm", zsines, real_y, precision=highest
    )
    spectrum = lax.psum_scatter(
        jnp.stack([term_real, term_imag], axis=1), "space", scatter_dimension=0, tiled=True
    )
    zangles = 2.0 * math.pi / grid_depth * zcells.astype(jnp.float32)
    yangles = 2.0 * math.pi / grid_rows * ymodes.astype(jnp.float32)
    xangles = 2.0 * math.pi / grid_cols * xmodes.astype(jnp.float32)
    keeper = (
        ((ymodes != -keep_y)[:, None] & (xmodes != -keep_x)[None, :])
        .astype(jnp.float32)
        .reshape(mode_count)
    )
    plane_cos = (
        (2.0 * jnp.cos(yangles) - 2.0)[:, None] + (2.0 * jnp.cos(xangles) - 2.0)[None, :]
    ).reshape(mode_count)
    plane_sin = (
        advect_yaxis * jnp.sin(yangles)[:, None] + advect_xaxis * jnp.sin(xangles)[None, :]
    ).reshape(mode_count)
    sym_real = (
        1.0 + diffusion_number * ((2.0 * jnp.cos(zangles) - 2.0)[:, None] + plane_cos[None, :])
    ) * keeper[None, :]
    sym_imag = -(advect_zaxis * jnp.sin(zangles)[:, None] + plane_sin[None, :]) * keeper[None, :]
    sym_real = sym_real[:, None, :]
    sym_imag = sym_imag[:, None, :]
    log_size = jnp.where(
        keeper[None, None, :] > 0.0,
        0.5 * jnp.log(sym_real * sym_real + sym_imag * sym_imag + (1.0 - keeper[None, None, :])),
        -60.0,
    )
    turning = jnp.arctan2(sym_imag, sym_real)
    fine_real = spectrum[:, 0, :fields]
    fine_imag = spectrum[:, 1, :fields]
    start_real = spectrum[:, 0, fields:]
    start_imag = spectrum[:, 1, fields:]
    position = lax.axis_index("tm")
    later_flag = (position > 0).astype(jnp.float32)
    coarse_real = sym_real * start_real - sym_imag * start_imag
    coarse_imag = sym_real * start_imag + sym_imag * start_real
    jumps = jnp.stack([fine_real - later_flag * coarse_real, fine_imag - later_flag * coarse_imag])
    portion = lax.all_gather(jumps[None], "tm", axis=0, tiled=True)
    source_rows = jnp.arange(portion.shape[0], dtype=jnp.int32)
    gaps = position - 1 - source_rows
    live = (gaps >= 0).astype(jnp.float32)[:, None, None, None]
    exponent = jnp.maximum(gaps, 0).astype(jnp.float32)[:, None, None, None]
    damping = live * jnp.exp(exponent * log_size[None])
    cosine = damping * jnp.cos(exponent * turning[None])
    sine_part = damping * jnp.sin(exponent * turning[None])
    added_real = jnp.sum(cosine * portion[:, 0] - sine_part * portion[:, 1], axis=0)
    added_imag = jnp.sum(cosine * portion[:, 1] + sine_part * portion[:, 0], axis=0)
    prior_sum = jnp.stack([added_real, added_imag])
    diff_real = prior_sum[0] - later_flag * start_real
    diff_imag = prior_sum[1] - later_flag * start_imag
    spectral_fix = jnp.stack(
        [sym_real * diff_real - sym_imag * diff_imag, sym_real * diff_imag + sym_imag * diff_real],
        axis=1,
    )
    portion = lax.all_gather(spectral_fix, "space", axis=0, tiled=True)
    zwaves = jnp.arange(portion.shape[0], dtype=jnp.int32)
    zcosines, zsines = wave_table(zcells, zwaves, grid_depth)
    back_real = jnp.einsum("zq,qfm->zfm", zcosines, portion[:, 0], precision=highest) - jnp.einsum(
        "zq,qfm->zfm", zsines, portion[:, 1], precision=highest
    )
    back_imag = jnp.einsum("zq,qfm->zfm", zcosines, portion[:, 1], precision=highest) + jnp.einsum(
        "zq,qfm->zfm", zsines, portion[:, 0], precision=highest
    )
    local_depth = jnp.stack([back_real, back_imag], axis=1)
    planes = local_depth.reshape(slab_depth, 2, fields, 2 * keep_y, 2 * keep_x)
    plane_real = jnp.einsum(
        "zfjk,yj->zfyk", planes[:, 0], ycosines, precision=highest
    ) - jnp.einsum("zfjk,yj->zfyk", planes[:, 1], ysines, precision=highest)
    plane_imag = jnp.einsum(
        "zfjk,yj->zfyk", planes[:, 1], ycosines, precision=highest
    ) + jnp.einsum("zfjk,yj->zfyk", planes[:, 0], ysines, precision=highest)
    correction = (
        jnp.einsum("zfyk,xk->fzyx", plane_real, xcosines, precision=highest)
        - jnp.einsum("zfyk,xk->fzyx", plane_imag, xsines, precision=highest)
    ) / (grid_depth * grid_rows * grid_cols)
    end_states = current + correction
    local_sum = jnp.sum(correction * correction)
    cell_total = fields * grid_depth * grid_rows * grid_cols
    slice_sum = lax.psum(local_sum, "space")
    every_sum = lax.psum(slice_sum, "tm")
    slice_value = jnp.sqrt(slice_sum / cell_total + epsilon).reshape(1)
    total_value = jnp.sqrt(every_sum / (cell_total * width_time) + epsilon).reshape(1)
    return (end_states[None], slice_value, total_value)


def solution(mesh):
    in_specs = (P("tm", None, "space", None, None), P(None, "space", None, None))
    out_specs = (P("tm", None, "space", None, None), P("tm"), P())
    return jax.shard_map(shards, mesh=mesh, in_specs=in_specs, out_specs=out_specs, check_vma=False)
```

profile of v0, /device:TPU:0, one launch (start us, length us, event | category | flops | bytes accessed | tf_op | source)
XLA Modules:
  0.0 202.2 jit_solution(17779550570251596355)
XLA Ops:
  7.2 1.8 fusion.450
  9.5 1.9 collective-permute-start.1
  24.0 1.2 dynamic-slice
  35.5 3.0 %collective-permute-done.2 = f32[5,1,64,128]{3,2,1,0:T(8,128)S(1)} collective-permute-done((f32[5,1,64,128]{3,2,1,0:T(8,128)S(1)}, f32[5,1,64,128]{3,2,1,0:T(8,128)S(1)}, u32[]{:S(2)}, u32[]{:S(2)}) %collective-permute-start.2) | collective-permute-done | bytes 163872 | tf_op jit(solution)/shard_map/ppermute | solution.py:26
  38.5 1.6 collective-permute-done.3
  45.0 1.4 collective-permute-start.5
  46.4 2.9 %collective-permute-done.4 = f32[5,1,64,128]{3,2,1,0:T(8,128)S(1)} collective-permute-done((f32[5,1,64,128]{3,2,1,0:T(8,128)S(1)}, f32[5,1,64,128]{3,2,1,0:T(8,128)S(1)}, u32[]{:S(2)}, u32[]{:S(2)}) %collective-permute-start.4) | collective-permute-done | bytes 163872 | tf_op jit(solution)/shard_map/ppermute | solution.py:26
  49.3 1.3 collective-permute-done.5
  56.1 1.3 collective-permute-start.7
  57.4 2.8 %collective-permute-done.6 = f32[5,1,64,128]{3,2,1,0:T(8,128)S(1)} collective-permute-done((f32[5,1,64,128]{3,2,1,0:T(8,128)S(1)}, f32[5,1,64,128]{3,2,1,0:T(8,128)S(1)}, u32[]{:S(2)}, u32[]{:S(2)}) %collective-permute-start.6) | collective-permute-done | bytes 163872 | tf_op jit(solution)/shard_map/ppermute | solution.py:26
  60.2 1.2 collective-permute-done.7
  64.5 3.2 %fusion.304 = f32[10,4,64,16]{2,3,1,0:T(8,128)S(1)} fusion(f32[10,4,64,128]{3,2,1,0:T(8,128)S(1)} %bitcast.754, s32[16]{0:T(128)S(1)} %compare_select_fusion), kind=kOutput, calls=%fused_computation.540 | convolution fusion | flops 62943232 | bytes 1474624 | tf_op jit(solution)/shard_map/bzyx,xk->bzyk/dot_general | solution.py:112
  67.7 3.2 %convolution_negate_fusion = f32[10,4,64,16]{2,3,1,0:T(8,128)S(1)} fusion(f32[10,4,64,128]{3,2,1,0:T(8,128)S(1)} %bitcast.755, s32[16]{0:T(128)S(1)} %compare_select_fusion), kind=kOutput, calls=%fused_computation.8 | convolution fusion | flops 62984192 | bytes 1474624 | tf_op jit(solution)/shard_map/bzyx,xk->bzyk/dot_general | solution.py:113
  70.9 2.5 %fusion.310 = f32[16,10,4,16]{3,0,2,1:T(8,128)S(1)} fusion(f32[10,4,64,16]{2,3,1,0:T(8,128)S(1)} %fusion.304, s32[16]{0:T(128)S(1)} %compare_select_fusion), kind=kOutput, calls=%fused_computation.546 | convolution fusion | flops 7878656 | bytes 204864 | tf_op jit(solution)/shard_map/bzyk,yj->bzjk/dot_general | solution.py:114
  73.4 2.5 %fusion.308 = f32[16,10,4,16]{3,0,2,1:T(8,128)S(1)} fusion(f32[10,4,64,16]{2,3,1,0:T(8,128)S(1)} %convolution_negate_fusion, s32[16]{0:T(128)S(1)} %compare_select_fusion), kind=kOutput, calls=%fused_computation.544 | convolution fusion | flops 7878656 | bytes 204864 | tf_op jit(solution)/shard_map/bzyk,yj->bzjk/dot_general | solution.py:117
  75.9 2.5 %fusion.3 = f32[10,4,16,16]{3,2,1,0:T(8,128)S(1)} fusion(f32[16,10,4,16]{3,0,2,1:T(8,128)S(1)} %fusion.310, f32[10,4,64,16]{2,3,1,0:T(8,128)S(1)} %convolution_negate_fusion, s32[16]{0:T(128)S(1)} %compare_select_fusion), kind=kOutput, calls=%fused_computation.7 | convolution fusion | flops 7888896 | bytes 245824 | tf_op jit(solution)/shard_map/bzyk,yj->bzjk/dot_general | solution.py:114
  78.6 2.5 %fusion.2 = f32[10,4,16,16]{3,2,1,0:T(8,128)S(1)} fusion(f32[16,10,4,16]{3,0,2,1:T(8,128)S(1)} %fusion.308, f32[10,4,64,16]{2,3,1,0:T(8,128)S(1)} %fusion.304, s32[16]{0:T(128)S(1)} %compare_select_fusion), kind=kOutput, calls=%fused_computation.5 | convolution fusion | flops 7888896 | bytes 245824 | tf_op jit(solution)/shard_map/bzyk,yj->bzjk/dot_general | solution.py:117
  84.4 32.7 %all-reduce.3.cloned.1.call-done = f32[16,2,10,256]{3,0,2,1:T(8,128)} async-done(((f32[16,2,10,256]{3,0,2,1:T(8,128)}), f32[16,2,10,256]{3,0,2,1:T(8,128)}) %all-reduce.3.cloned.1.call-update) | async-done | bytes 327696
  118.0 31.1 %all-gather = f32[16,4,5,256]{3,1,2,0:T(4,128)S(1)} all-gather(f32[2,4,5,256]{3,1,2,0:T(4,128)S(1)} %pad_maximum_fusion.26), channel_id=2, replica_groups=mesh['tm'=8,'space'=4] {'tm'}, dimensions={0}, use_global_device_ids=true | all-gather | bytes 368640 | tf_op jit(solution)/shard_map/all_gather | solution.py:170
  150.1 5.7 %all_gather.7 = f32[16,2,5,256]{3,1,2,0:T(2,128)S(1)} all-gather(f32[4,2,5,256]{3,1,2,0:T(2,128)S(1)} %copy.243), channel_id=1, replica_groups=mesh['tm'=8,'space'=4] {'space'}, dimensions={0}, use_global_device_ids=true | all-gather | bytes 204800 | tf_op jit(solution)/shard_map/all_gather | solution.py:187
  159.3 1.2 fusion.302
  160.5 1.8 multiply_reduce_fusion
  162.4 6.6 %psum.14 = f32[]{:T(128)} all-reduce(f32[]{:T(128)} %get-tuple-element.60), channel_id=1, replica_groups=mesh['tm'=8,'space'=4] {'space'}, use_global_device_ids=true, to_apply=%region_4.5 | all-reduce | flops 1 | bytes 8 | tf_op jit(solution)/shard_map/psum | solution.py:211
  169.9 21.8 %psum.15 = f32[]{:T(128)} all-reduce(f32[]{:T(128)} %psum.14), channel_id=1, replica_groups=mesh['tm'=8,'space'=4] {'tm'}, use_global_device_ids=true, to_apply=%region_5.6 | all-reduce | flops 1 | bytes 8 | tf_op jit(solution)/shard_map/psum | solution.py:212
  (269 shorter events, 44.4 us)
Async XLA Ops:
  7.2 110.0 %all-reduce.3.cloned.1.call-start = ((), (), s32[]{:S(2)}) async-start(), calls=%async_computation | async-start | bytes 655360
  9.0 17.5 %collective-permute-start = (f32[5,1,64,128]{3,2,1,0:T(8,128)}, f32[5,1,64,128]{3,2,1,0:T(8,128)S(1)}, u32[]{:S(2)}, u32[]{:S(2)}) collective-permute-start(f32[5,1,64,128]{3,2,1,0:T(8,128)} %get-tuple-element.91), channel_id=1, source_target_pairs={{0,1},{1,2},{2,3},{3,0},{4,5},{5,6},{6,7},{7,4},{8,9},{9,10},{10,1... | collective-permute-start | bytes 491528 | tf_op jit(solution)/shard_map/ppermute | solution.py:26
  9.5 17.0 %collective-permute-start.1 = (f32[5,1,64,128]{3,2,1,0:T(8,128)}, f32[5,1,64,128]{3,2,1,0:T(8,128)S(1)}, u32[]{:S(2)}, u32[]{:S(2)}) collective-permute-start(f32[5,1,64,128]{3,2,1,0:T(8,128)} %get-tuple-element.90), channel_id=1, source_target_pairs={{1,0},{2,1},{3,2},{0,3},{5,4},{6,5},{7,6},{4,7},{9,8},{10,9},{11,1... | collective-permute-start | bytes 491528 | tf_op jit(solution)/shard_map/ppermute | solution.py:28
  16.0 10.4 %copy-start = (f32[1,5,4,64,128]{4,3,2,1,0:T(8,128)S(1)}, f32[1,5,4,64,128]{4,3,2,1,0:T(8,128)}, u32[]{:S(2)}) copy-start(f32[1,5,4,64,128]{4,3,2,1,0:T(8,128)} %param.2) | copy-start | bytes 1966084
  27.6 1.0 copy-start.9
  27.7 1.1 copy-start.10
  27.7 1.1 copy-start.11
  27.7 1.2 copy-start.12
  28.8 1.0 copy-start.4
  28.8 1.1 copy-start.5
  28.9 1.2 copy-start.6
  30.0 1.0 copy-start.14
  30.0 1.0 copy-start.15
  30.0 1.1 copy-start.16
  30.0 1.2 copy-start.17
  30.0 1.2 copy-start.18
  31.4 1.1 copy-start.1
  33.7 4.8 %collective-permute-start.2 = (f32[5,1,64,128]{3,2,1,0:T(8,128)S(1)}, f32[5,1,64,128]{3,2,1,0:T(8,128)S(1)}, u32[]{:S(2)}, u32[]{:S(2)}) collective-permute-start(f32[5,1,64,128]{3,2,1,0:T(8,128)S(1)} %get-tuple-element.84), channel_id=1, source_target_pairs={{0,1},{1,2},{2,3},{3,0},{4,5},{5,6},{6,7},{7,4},{8,9},{9,10},{10,1... | collective-permute-start | bytes 491528 | tf_op jit(solution)/shard_map/ppermute | solution.py:26
  34.4 5.7 %collective-permute-start.3 = (f32[5,1,64,128]{3,2,1,0:T(8,128)S(1)}, f32[5,1,64,128]{3,2,1,0:T(8,128)S(1)}, u32[]{:S(2)}, u32[]{:S(2)}) collective-permute-start(f32[5,1,64,128]{3,2,1,0:T(8,128)S(1)} %get-tuple-element.83), channel_id=1, source_target_pairs={{1,0},{2,1},{3,2},{0,3},{5,4},{6,5},{7,6},{4,7},{9,8},{10,9},{11,1... | collective-permute-start | bytes 491528 | tf_op jit(solution)/shard_map/ppermute | solution.py:28
  44.1 5.2 %collective-permute-start.4 = (f32[5,1,64,128]{3,2,1,0:T(8,128)S(1)}, f32[5,1,64,128]{3,2,1,0:T(8,128)S(1)}, u32[]{:S(2)}, u32[]{:S(2)}) collective-permute-start(f32[5,1,64,128]{3,2,1,0:T(8,128)S(1)} %get-tuple-element.76), channel_id=1, source_target_pairs={{0,1},{1,2},{2,3},{3,0},{4,5},{5,6},{6,7},{7,4},{8,9},{9,10},{10,1... | collective-permute-start | bytes 491528 | tf_op jit(solution)/shard_map/ppermute | solution.py:26
  45.0 5.6 %collective-permute-start.5 = (f32[5,1,64,128]{3,2,1,0:T(8,128)S(1)}, f32[5,1,64,128]{3,2,1,0:T(8,128)S(1)}, u32[]{:S(2)}, u32[]{:S(2)}) collective-permute-start(f32[5,1,64,128]{3,2,1,0:T(8,128)S(1)} %get-tuple-element.75), channel_id=1, source_target_pairs={{1,0},{2,1},{3,2},{0,3},{5,4},{6,5},{7,6},{4,7},{9,8},{10,9},{11,1... | collective-permute-start | bytes 491528 | tf_op jit(solution)/shard_map/ppermute | solution.py:28
  55.2 5.0 %collective-permute-start.6 = (f32[5,1,64,128]{3,2,1,0:T(8,128)S(1)}, f32[5,1,64,128]{3,2,1,0:T(8,128)S(1)}, u32[]{:S(2)}, u32[]{:S(2)}) collective-permute-start(f32[5,1,64,128]{3,2,1,0:T(8,128)S(1)} %get-tuple-element.68), channel_id=1, source_target_pairs={{0,1},{1,2},{2,3},{3,0},{4,5},{5,6},{6,7},{7,4},{8,9},{9,10},{10,1... | collective-permute-start | bytes 491528 | tf_op jit(solution)/shard_map/ppermute | solution.py:26
  56.1 5.3 %collective-permute-start.7 = (f32[5,1,64,128]{3,2,1,0:T(8,128)S(1)}, f32[5,1,64,128]{3,2,1,0:T(8,128)S(1)}, u32[]{:S(2)}, u32[]{:S(2)}) collective-permute-start(f32[5,1,64,128]{3,2,1,0:T(8,128)S(1)} %get-tuple-element.67), channel_id=1, source_target_pairs={{1,0},{2,1},{3,2},{0,3},{5,4},{6,5},{7,6},{4,7},{9,8},{10,9},{11,1... | collective-permute-start | bytes 491528 | tf_op jit(solution)/shard_map/ppermute | solution.py:28
  81.1 3.0 %copy-start.19 = (f32[8]{0:T(128)S(1)}, f32[8]{0:T(128)}, u32[]{:S(2)}) copy-start(f32[8]{0:T(128)} %maximum_convert_fusion) | copy-start | bytes 100
  (5 other events, 4.6 us)
Sparse Core Ops, SparseCore 0:
  84.2 32.9 all-reduce.2
where the time goes:
time: 203 us; the launch traced here: 202 us
  blocking collectives  65.3 us (32%)
  waiting for transfers between devices  45.6 us (22%)
  matrix products  24.5 us (12%)
  local copies, waits for them, and re-layouts  22.2 us (11%)
  between operations  19.9 us (10%)
  other arithmetic  16 us (8%)
  starting transfers between devices  8.72 us (4%)
    unnamed x2, waiting for transfers between devices  32.7 us
    all_gather x1, blocking collectives, shards(): portion = lax.all_gather(jumps[None], 'tm', axis=0, tiled=True)  31.1 us
    psum x1, blocking collectives, shards(): every_sum = lax.psum(slice_sum, 'tm')  21.8 us
    ppermute x4, waiting for transfers between devices, with_halo(): lax.ppermute(tail, axis, [(i, (i + 1) % count) for i in range(count)])  8.68 us
    psum x1, blocking collectives, shards(): slice_sum = lax.psum(local_sum, 'space')  6.61 us
    all_gather x1, blocking collectives, shards(): portion = lax.all_gather(spectral_fix, 'space', axis=0, tiled=True)  5.73 us
    ppermute x4, starting transfers between devices, with_halo(): lax.ppermute(head, axis, [((i + 1) % count, i) for i in range(count)])  5.7 us
    unnamed x42, local copies, waits for them, and re-layouts  5.61 us
  transfers between devices with their start and end apart: 9, of which 7 were waited for; matrix products, arithmetic and copies ran while one was open for 7% of the time, Pallas kernels for 0%

commit v1 on v0

--- a/solution.py
+++ b/solution.py
@@ -209,7 +209,11 @@
     local_sum = jnp.sum(correction * correction)
     cell_total = fields * grid_depth * grid_rows * grid_cols
     slice_sum = lax.psum(local_sum, "space")
-    every_sum = lax.psum(slice_sum, "tm")
+    every_sum = slice_sum
+    for hop in (1, 2, 4):
+        every_sum = every_sum + lax.ppermute(
+            every_sum, "tm", [(dev, dev ^ hop) for dev in range(8)]
+        )
     slice_value = jnp.sqrt(slice_sum / cell_total + epsilon).reshape(1)
     total_value = jnp.sqrt(every_sum / (cell_total * width_time) + epsilon).reshape(1)
     return (end_states[None], slice_value, total_value)

time: 203 us -> 193 us (0.951)
  blocking collectives: 65.3 us -> 43.4 us
  starting transfers between devices: 8.72 us -> 14.1 us
  waiting for transfers between devices: 45.6 us -> 50.8 us
    psum x1 -> x0, blocking collectives: 21.8 us -> none  [shards(): every_sum = lax.psum(slice_sum, 'tm')]
    ppermute x0 -> x3, starting transfers between devices: none -> 5.35 us  [shards(): lax.ppermute(every_sum, 'tm', [(dev, dev ^ hop) for dev in range(8)])]
    ppermute x0 -> x3, waiting for transfers between devices: none -> 5.25 us  [shards(): lax.ppermute(every_sum, 'tm', [(dev, dev ^ hop) for dev in range(8)])]
  transfers between devices with their start and end apart: 9 -> 12, of which waited for: 7 -> 10; matrix products, arithmetic and copies ran while one was open for 7% -> 8% of each run, Pallas kernels for 0% -> 0%
where the time goes in v1:
time: 193 us; the launch traced here: 192 us
  waiting for transfers between devices  50.8 us (26%)
  blocking collectives  43.4 us (22%)
  matrix products  24.5 us (13%)
  local copies, waits for them, and re-layouts  22.2 us (12%)
  between operations  21.6 us (11%)
  other arithmetic  15.8 us (8%)
  starting transfers between devices  14.1 us (7%)
    unnamed x2, waiting for transfers between devices  32.8 us
    all_gather x1, blocking collectives, shards(): portion = lax.all_gather(jumps[None], 'tm', axis=0, tiled=True)  31.1 us
    ppermute x4, waiting for transfers between devices, with_halo(): lax.ppermute(tail, axis, [(i, (i + 1) % count) for i in range(count)])  8.68 us
    psum x1, blocking collectives, shards(): slice_sum = lax.psum(local_sum, 'space')  6.61 us
    all_gather x1, blocking collectives, shards(): portion = lax.all_gather(spectral_fix, 'space', axis=0, tiled=True)  5.73 us
    ppermute x4, starting transfers between devices, with_halo(): lax.ppermute(head, axis, [((i + 1) % count, i) for i in range(count)])  5.7 us
    unnamed x42, local copies, waits for them, and re-layouts  5.61 us
    ppermute x3, starting transfers between devices, shards(): lax.ppermute(every_sum, 'tm', [(dev, dev ^ hop) for dev in range(8)])  5.35 us
  transfers between devices with their start and end apart: 12, of which 10 were waited for; matrix products, arithmetic and copies ran while one was open for 8% of the time, Pallas kernels for 0%

profile of v1, /device:TPU:0, one launch (start us, length us, event | category | flops | bytes accessed | tf_op | source)
XLA Modules:
  0.0 192.4 jit_solution(10039134884684870298)
XLA Ops:
  7.2 1.7 fusion.450
  9.5 1.9 collective-permute-start.1
  35.3 3.0 %collective-permute-done.2 = f32[5,1,64,128]{3,2,1,0:T(8,128)S(1)} collective-permute-done((f32[5,1,64,128]{3,2,1,0:T(8,128)S(1)}, f32[5,1,64,128]{3,2,1,0:T(8,128)S(1)}, u32[]{:S(2)}, u32[]{:S(2)}) %collective-permute-start.2) | collective-permute-done | bytes 163872 | tf_op jit(solution)/shard_map/ppermute | solution.py:26
  38.3 1.6 collective-permute-done.3
  44.8 1.4 collective-permute-start.5
  46.2 2.9 %collective-permute-done.4 = f32[5,1,64,128]{3,2,1,0:T(8,128)S(1)} collective-permute-done((f32[5,1,64,128]{3,2,1,0:T(8,128)S(1)}, f32[5,1,64,128]{3,2,1,0:T(8,128)S(1)}, u32[]{:S(2)}, u32[]{:S(2)}) %collective-permute-start.4) | collective-permute-done | bytes 163872 | tf_op jit(solution)/shard_map/ppermute | solution.py:26
  55.9 1.3 collective-permute-start.7
  57.2 2.8 %collective-permute-done.6 = f32[5,1,64,128]{3,2,1,0:T(8,128)S(1)} collective-permute-done((f32[5,1,64,128]{3,2,1,0:T(8,128)S(1)}, f32[5,1,64,128]{3,2,1,0:T(8,128)S(1)}, u32[]{:S(2)}, u32[]{:S(2)}) %collective-permute-start.6) | collective-permute-done | bytes 163872 | tf_op jit(solution)/shard_map/ppermute | solution.py:26
  64.3 3.2 %fusion.304 = f32[10,4,64,16]{2,3,1,0:T(8,128)S(1)} fusion(f32[10,4,64,128]{3,2,1,0:T(8,128)S(1)} %bitcast.754, s32[16]{0:T(128)S(1)} %compare_select_fusion), kind=kOutput, calls=%fused_computation.540 | convolution fusion | flops 62943232 | bytes 1474624 | tf_op jit(solution)/shard_map/bzyx,xk->bzyk/dot_general | solution.py:112
  67.5 3.2 %convolution_negate_fusion = f32[10,4,64,16]{2,3,1,0:T(8,128)S(1)} fusion(f32[10,4,64,128]{3,2,1,0:T(8,128)S(1)} %bitcast.755, s32[16]{0:T(128)S(1)} %compare_select_fusion), kind=kOutput, calls=%fused_computation.8 | convolution fusion | flops 62984192 | bytes 1474624 | tf_op jit(solution)/shard_map/bzyx,xk->bzyk/dot_general | solution.py:113
  70.7 2.5 %fusion.310 = f32[16,10,4,16]{3,0,2,1:T(8,128)S(1)} fusion(f32[10,4,64,16]{2,3,1,0:T(8,128)S(1)} %fusion.304, s32[16]{0:T(128)S(1)} %compare_select_fusion), kind=kOutput, calls=%fused_computation.546 | convolution fusion | flops 7878656 | bytes 204864 | tf_op jit(solution)/shard_map/bzyk,yj->bzjk/dot_general | solution.py:114
  73.2 2.5 %fusion.308 = f32[16,10,4,16]{3,0,2,1:T(8,128)S(1)} fusion(f32[10,4,64,16]{2,3,1,0:T(8,128)S(1)} %convolution_negate_fusion, s32[16]{0:T(128)S(1)} %compare_select_fusion), kind=kOutput, calls=%fused_computation.544 | convolution fusion | flops 7878656 | bytes 204864 | tf_op jit(solution)/shard_map/bzyk,yj->bzjk/dot_general | solution.py:117
  75.7 2.5 %fusion.3 = f32[10,4,16,16]{3,2,1,0:T(8,128)S(1)} fusion(f32[16,10,4,16]{3,0,2,1:T(8,128)S(1)} %fusion.310, f32[10,4,64,16]{2,3,1,0:T(8,128)S(1)} %convolution_negate_fusion, s32[16]{0:T(128)S(1)} %compare_select_fusion), kind=kOutput, calls=%fused_computation.7 | convolution fusion | flops 7888896 | bytes 245824 | tf_op jit(solution)/shard_map/bzyk,yj->bzjk/dot_general | solution.py:114
  78.3 2.5 %fusion.2 = f32[10,4,16,16]{3,2,1,0:T(8,128)S(1)} fusion(f32[16,10,4,16]{3,0,2,1:T(8,128)S(1)} %fusion.308, f32[10,4,64,16]{2,3,1,0:T(8,128)S(1)} %fusion.304, s32[16]{0:T(128)S(1)} %compare_select_fusion), kind=kOutput, calls=%fused_computation.5 | convolution fusion | flops 7888896 | bytes 245824 | tf_op jit(solution)/shard_map/bzyk,yj->bzjk/dot_general | solution.py:117
  84.2 32.7 %all-reduce.3.cloned.1.call-done = f32[16,2,10,256]{3,0,2,1:T(8,128)} async-done(((f32[16,2,10,256]{3,0,2,1:T(8,128)}), f32[16,2,10,256]{3,0,2,1:T(8,128)}) %all-reduce.3.cloned.1.call-update) | async-done | bytes 327696
  117.8 31.1 %all-gather = f32[16,4,5,256]{3,1,2,0:T(4,128)S(1)} all-gather(f32[2,4,5,256]{3,1,2,0:T(4,128)S(1)} %pad_maximum_fusion.26), channel_id=2, replica_groups=mesh['tm'=8,'space'=4] {'tm'}, dimensions={0}, use_global_device_ids=true | all-gather | bytes 368640 | tf_op jit(solution)/shard_map/all_gather | solution.py:170
  149.9 5.7 %all_gather.7 = f32[16,2,5,256]{3,1,2,0:T(2,128)S(1)} all-gather(f32[4,2,5,256]{3,1,2,0:T(2,128)S(1)} %copy.243), channel_id=1, replica_groups=mesh['tm'=8,'space'=4] {'space'}, dimensions={0}, use_global_device_ids=true | all-gather | bytes 204800 | tf_op jit(solution)/shard_map/all_gather | solution.py:187
  160.3 1.8 multiply_reduce_fusion
  162.2 6.6 %psum.7 = f32[]{:T(128)} all-reduce(f32[]{:T(128)} %get-tuple-element.60), channel_id=1, replica_groups=mesh['tm'=8,'space'=4] {'space'}, use_global_device_ids=true, to_apply=%region_4.5 | all-reduce | flops 1 | bytes 8 | tf_op jit(solution)/shard_map/psum | solution.py:211
  168.8 1.4 collective-permute-start.8
  173.8 1.4 collective-permute-start.9
  175.1 2.4 %collective-permute-done.9 = f32[]{:T(128)} collective-permute-done((f32[]{:T(128)}, f32[]{:T(128)}, u32[]{:S(2)}, u32[]{:S(2)}) %collective-permute-start.9) | collective-permute-done | bytes 36 | tf_op jit(solution)/shard_map/ppermute | solution.py:214
  178.1 2.6 %collective-permute-start.10 = (f32[]{:T(128)}, f32[]{:T(128)}, u32[]{:S(2)}, u32[]{:S(2)}) collective-permute-start(f32[]{:T(128)} %add.1092), channel_id=1, source_target_pairs={{0,16},{4,20},{8,24},{12,28},{16,0},{20,4},{24,8},{28,12},{1,17},{... | collective-permute-start | bytes 20 | tf_op jit(solution)/shard_map/ppermute | solution.py:214
  180.6 2.1 %collective-permute-done.10 = f32[]{:T(128)} collective-permute-done((f32[]{:T(128)}, f32[]{:T(128)}, u32[]{:S(2)}, u32[]{:S(2)}) %collective-permute-start.10) | collective-permute-done | bytes 36 | tf_op jit(solution)/shard_map/ppermute | solution.py:214
  (274 shorter events, 50.0 us)
Async XLA Ops:
  7.2 109.7 %all-reduce.3.cloned.1.call-start = ((), (), s32[]{:S(2)}) async-start(), calls=%async_computation | async-start | bytes 655360
  9.0 17.2 %collective-permute-start = (f32[5,1,64,128]{3,2,1,0:T(8,128)}, f32[5,1,64,128]{3,2,1,0:T(8,128)S(1)}, u32[]{:S(2)}, u32[]{:S(2)}) collective-permute-start(f32[5,1,64,128]{3,2,1,0:T(8,128)} %get-tuple-element.91), channel_id=1, source_target_pairs={{0,1},{1,2},{2,3},{3,0},{4,5},{5,6},{6,7},{7,4},{8,9},{9,10},{10,1... | collective-permute-start | bytes 491528 | tf_op jit(solution)/shard_map/ppermute | solution.py:26
  9.5 16.7 %collective-permute-start.1 = (f32[5,1,64,128]{3,2,1,0:T(8,128)}, f32[5,1,64,128]{3,2,1,0:T(8,128)S(1)}, u32[]{:S(2)}, u32[]{:S(2)}) collective-permute-start(f32[5,1,64,128]{3,2,1,0:T(8,128)} %get-tuple-element.90), channel_id=1, source_target_pairs={{1,0},{2,1},{3,2},{0,3},{5,4},{6,5},{7,6},{4,7},{9,8},{10,9},{11,1... | collective-permute-start | bytes 491528 | tf_op jit(solution)/shard_map/ppermute | solution.py:28
  16.0 10.2 %copy-start = (f32[1,5,4,64,128]{4,3,2,1,0:T(8,128)S(1)}, f32[1,5,4,64,128]{4,3,2,1,0:T(8,128)}, u32[]{:S(2)}) copy-start(f32[1,5,4,64,128]{4,3,2,1,0:T(8,128)} %param.2) | copy-start | bytes 1966084
  27.4 1.1 copy-start.10
  27.4 1.1 copy-start.11
  27.4 1.2 copy-start.12
  28.6 1.0 copy-start.4
  28.6 1.1 copy-start.5
  28.6 1.2 copy-start.6
  29.8 1.1 copy-start.16
  29.8 1.2 copy-start.17
  29.8 1.2 copy-start.18
  31.1 1.1 copy-start.1
  33.5 4.8 %collective-permute-start.2 = (f32[5,1,64,128]{3,2,1,0:T(8,128)S(1)}, f32[5,1,64,128]{3,2,1,0:T(8,128)S(1)}, u32[]{:S(2)}, u32[]{:S(2)}) collective-permute-start(f32[5,1,64,128]{3,2,1,0:T(8,128)S(1)} %get-tuple-element.84), channel_id=1, source_target_pairs={{0,1},{1,2},{2,3},{3,0},{4,5},{5,6},{6,7},{7,4},{8,9},{9,10},{10,1... | collective-permute-start | bytes 491528 | tf_op jit(solution)/shard_map/ppermute | solution.py:26
  34.2 5.7 %collective-permute-start.3 = (f32[5,1,64,128]{3,2,1,0:T(8,128)S(1)}, f32[5,1,64,128]{3,2,1,0:T(8,128)S(1)}, u32[]{:S(2)}, u32[]{:S(2)}) collective-permute-start(f32[5,1,64,128]{3,2,1,0:T(8,128)S(1)} %get-tuple-element.83), channel_id=1, source_target_pairs={{1,0},{2,1},{3,2},{0,3},{5,4},{6,5},{7,6},{4,7},{9,8},{10,9},{11,1... | collective-permute-start | bytes 491528 | tf_op jit(solution)/shard_map/ppermute | solution.py:28
  43.9 5.2 %collective-permute-start.4 = (f32[5,1,64,128]{3,2,1,0:T(8,128)S(1)}, f32[5,1,64,128]{3,2,1,0:T(8,128)S(1)}, u32[]{:S(2)}, u32[]{:S(2)}) collective-permute-start(f32[5,1,64,128]{3,2,1,0:T(8,128)S(1)} %get-tuple-element.76), channel_id=1, source_target_pairs={{0,1},{1,2},{2,3},{3,0},{4,5},{5,6},{6,7},{7,4},{8,9},{9,10},{10,1... | collective-permute-start | bytes 491528 | tf_op jit(solution)/shard_map/ppermute | solution.py:26
  44.8 5.6 %collective-permute-start.5 = (f32[5,1,64,128]{3,2,1,0:T(8,128)S(1)}, f32[5,1,64,128]{3,2,1,0:T(8,128)S(1)}, u32[]{:S(2)}, u32[]{:S(2)}) collective-permute-start(f32[5,1,64,128]{3,2,1,0:T(8,128)S(1)} %get-tuple-element.75), channel_id=1, source_target_pairs={{1,0},{2,1},{3,2},{0,3},{5,4},{6,5},{7,6},{4,7},{9,8},{10,9},{11,1... | collective-permute-start | bytes 491528 | tf_op jit(solution)/shard_map/ppermute | solution.py:28
  55.0 5.0 %collective-permute-start.6 = (f32[5,1,64,128]{3,2,1,0:T(8,128)S(1)}, f32[5,1,64,128]{3,2,1,0:T(8,128)S(1)}, u32[]{:S(2)}, u32[]{:S(2)}) collective-permute-start(f32[5,1,64,128]{3,2,1,0:T(8,128)S(1)} %get-tuple-element.68), channel_id=1, source_target_pairs={{0,1},{1,2},{2,3},{3,0},{4,5},{5,6},{6,7},{7,4},{8,9},{9,10},{10,1... | collective-permute-start | bytes 491528 | tf_op jit(solution)/shard_map/ppermute | solution.py:26
  55.9 5.3 %collective-permute-start.7 = (f32[5,1,64,128]{3,2,1,0:T(8,128)S(1)}, f32[5,1,64,128]{3,2,1,0:T(8,128)S(1)}, u32[]{:S(2)}, u32[]{:S(2)}) collective-permute-start(f32[5,1,64,128]{3,2,1,0:T(8,128)S(1)} %get-tuple-element.67), channel_id=1, source_target_pairs={{1,0},{2,1},{3,2},{0,3},{5,4},{6,5},{7,6},{4,7},{9,8},{10,9},{11,1... | collective-permute-start | bytes 491528 | tf_op jit(solution)/shard_map/ppermute | solution.py:28
  80.8 3.0 %copy-start.19 = (f32[8]{0:T(128)S(1)}, f32[8]{0:T(128)}, u32[]{:S(2)}) copy-start(f32[8]{0:T(128)} %maximum_convert_fusion) | copy-start | bytes 100
  168.8 3.8 %collective-permute-start.8 = (f32[]{:T(128)}, f32[]{:T(128)}, u32[]{:S(2)}, u32[]{:S(2)}) collective-permute-start(f32[]{:T(128)} %psum.7), channel_id=1, source_target_pairs={{0,4},{4,0},{8,12},{12,8},{16,20},{20,16},{24,28},{28,24},{1,5},{5... | collective-permute-start | bytes 20 | tf_op jit(solution)/shard_map/ppermute | solution.py:214
  173.8 3.7 %collective-permute-start.9 = (f32[]{:T(128)}, f32[]{:T(128)}, u32[]{:S(2)}, u32[]{:S(2)}) collective-permute-start(f32[]{:T(128)} %add.1091), channel_id=1, source_target_pairs={{0,8},{4,12},{8,0},{12,4},{16,24},{20,28},{24,16},{28,20},{1,9},{5... | collective-permute-start | bytes 20 | tf_op jit(solution)/shard_map/ppermute | solution.py:214
  178.1 4.6 %collective-permute-start.10 = (f32[]{:T(128)}, f32[]{:T(128)}, u32[]{:S(2)}, u32[]{:S(2)}) collective-permute-start(f32[]{:T(128)} %add.1092), channel_id=1, source_target_pairs={{0,16},{4,20},{8,24},{12,28},{16,0},{20,4},{24,8},{28,12},{1,17},{... | collective-permute-start | bytes 20 | tf_op jit(solution)/shard_map/ppermute | solution.py:214
  (8 other events, 7.6 us)
Sparse Core Ops, SparseCore 0:
  84.0 32.9 all-reduce.2
